TPU v7x, 32 devices: a whole 2x2x4 slice. The times are simulated.
32 devices in a mesh: dp: 8 (over y, x, core), mp: 4 (over z).
Axes of the slice: x: 2, y: 2, z: 4, core: 2. Of those that a mesh axis runs over, the one named last changes fastest.
Arguments:
- feature_ids: int32 [8, 2048, 8], P('dp'), may hold values from 0 to 4095
- tables: bfloat16 [8, 4096, 128], P('dp'), may hold values from -5 to 5
- table_of_feature: int32 [8], replicated, may hold values from 0 to 7, each once
- cross_down: bfloat16 [2, 1024, 512], P(None, 'mp'), may hold values from -0.1875 to 0.1875
- cross_up: bfloat16 [2, 1024, 512], P(None, 'mp'), may hold values from -0.125 to 0.125
- cross_bias: float32 [2, 1024], P(None, 'mp'), may hold values from -3 to 3
- tower_weight: bfloat16 [1024, 2048], P('dp', 'mp'), may hold values from -0.1875 to 0.1875
- tower_bias: float32 [2048], P('mp'), may hold values from -3 to 3
Outputs:
- hidden: bfloat16 [2048, 2048], P('dp', 'mp')
Inputs may be any that keep to these rules, and one draw needn't show every extreme that they name: `feature_ids`: each id indexes a row of its own table. `table_of_feature`: each table serves exactly one feature.
All inputs are finite; a program needn't handle non-finite values.
Results may differ from a plain program's by a relative error of at most 0.015.
Values may be sent and summed in bfloat16 or wider, within the bound.
A program may use at most 64 MiB of HBM per device.

v0:
```python
import jax
import jax.numpy as jnp
from jax import lax
from jax.sharding import PartitionSpec as P


def body(
    feature_ids,
    tables,
    table_of_feature,
    cross_down,
    cross_up,
    cross_bias,
    tower_weight,
    tower_bias,
):
    groups = lax.axis_size("dp")
    members = lax.axis_size("mp")
    member = lax.axis_index("mp")
    table_count, batch_size, hot_count = feature_ids.shape
    row_count = batch_size // (groups * members)
    shaped = feature_ids[0].reshape(groups, members, row_count, hot_count)
    own_ids = lax.dynamic_index_in_dim(shaped, member, 1, keepdims=False).reshape(
        groups * row_count, hot_count
    )
    summed = jnp.zeros((groups * row_count, tables.shape[2]), jnp.float32)
    for hot_index in range(hot_count):
        summed = summed + jnp.take(tables[0], own_ids[:, hot_index], axis=0).astype(jnp.float32)
    columns = [summed.astype(jnp.bfloat16)]
    pooled = jnp.stack(columns, axis=1)
    regrouped = lax.all_to_all(pooled, "dp", split_axis=0, concat_axis=1, tiled=True)
    ordered = jnp.take(regrouped, table_of_feature, axis=1)
    by_width = lax.all_to_all(ordered, "mp", split_axis=1, concat_axis=0, tiled=True)
    group_rows = by_width.shape[0]
    embedded = by_width.reshape(group_rows, -1)
    embedded_wide = embedded.astype(jnp.float32)
    crossed = embedded
    layer_total = cross_down.shape[0]
    for layer_index in range(layer_total):
        partial_value = jnp.dot(
            crossed, cross_down[layer_index], preferred_element_type=jnp.float32
        )
        projected = lax.psum(partial_value.astype(jnp.bfloat16), "mp")
        lifted = lax.dot_general(
            projected,
            cross_up[layer_index],
            (((1,), (1,)), ((), ())),
            preferred_element_type=jnp.float32,
        )
        crossed = (
            embedded_wide * (lifted + cross_bias[layer_index]) + crossed.astype(jnp.float32)
        ).astype(jnp.bfloat16)
    full_rows = lax.all_gather(crossed, "mp", axis=1, tiled=True)
    pre_act = jnp.dot(
        full_rows,
        lax.all_gather(tower_weight, "dp", axis=0, tiled=True),
        preferred_element_type=jnp.float32,
    )
    return jax.nn.relu(pre_act + tower_bias).astype(jnp.bfloat16)


def solution(mesh):
    return jax.shard_map(
        body,
        mesh=mesh,
        in_specs=(
            P("dp", None, None),
            P("dp", None, None),
            P(),
            P(None, "mp", None),
            P(None, "mp", None),
            P(None, "mp"),
            P("dp", "mp"),
            P("mp"),
        ),
        out_specs=P("dp", "mp"),
        check_vma=False,
    )
```

profile of v0, /device:TPU:0, one launch (start us, length us, event | category | flops | bytes accessed | tf_op | source)
XLA Modules:
  0.0 143.6 jit_solution(9518459660529289800)
XLA Ops:
  7.4 1.0 reshape_squeeze.3
  8.4 0.1 dynamic-slice_reduce_fusion
  8.5 0.1 reshape.19
  8.8 1.3 gather_fusion.2
  10.2 1.3 gather_fusion.3
  11.5 1.3 gather_fusion.4
  12.9 1.3 gather_fusion.5
  14.2 1.3 gather_fusion.6
  15.6 1.3 gather_fusion.7
  17.0 1.3 gather_fusion.8
  18.3 1.3 gather_fusion.1
  19.7 0.8 fusion.16
  20.5 0.5 broadcast.59
  21.0 0.7 reduce.4
  21.7 0.7 reshape.125
  22.3 5.3 %all-to-all-start = ((bf16[8,2,4096]{2,1,0:T(2,128)(2,1)}), bf16[8,2,4096]{2,1,0:T(2,128)(2,1)S(1)}, u32[]{:S(2)}, u32[]{:S(2)}) async-start(bf16[8,2,4096]{2,1,0:T(2,128)(2,1)} %reshape.125), calls=%async_computation | async-start | bytes 262144 | tf_op jit(solution)/shard_map/all_to_all | solution.py:31
  27.8 5.4 %all-to-all-done = bf16[8,2,4096]{2,1,0:T(2,128)(2,1)S(1)} async-done(((bf16[8,2,4096]{2,1,0:T(2,128)(2,1)}), bf16[8,2,4096]{2,1,0:T(2,128)(2,1)S(1)}, u32[]{:S(2)}, u32[]{:S(2)}) %all-to-all-start) | async-done | bytes 131104 | tf_op jit(solution)/shard_map/all_to_all | solution.py:31
  33.2 0.1 reshape.126
  33.3 0.6 gather_fusion
  33.9 0.1 select_bitcast_fusion
  34.0 10.6 %all_to_all.33 = bf16[64,8,128]{2,0,1:T(8,128)(2,1)S(1)} all-to-all(bf16[64,8,128]{2,0,1:T(8,128)(2,1)S(1)} %select_bitcast_fusion), channel_id=1, replica_groups=mesh['dp'=8,'mp'=4] {'mp'}, dimensions={1} | all-to-all | bytes 262144 | tf_op jit(solution)/shard_map/all_to_all | solution.py:33
  44.6 0.1 copy.13
  44.8 0.9 convolution_convert_fusion.1
  45.8 0.6 copy-done.2
  46.4 32.4 %all-reduce.3.cloned.1.call-done = bf16[256,512]{1,0:T(8,128)(2,1)} async-done(((bf16[256,512]{1,0:T(8,128)(2,1)}), bf16[256,512]{1,0:T(8,128)(2,1)}) %all-reduce.3.cloned.1.call-update) | async-done | bytes 262160 | tf_op jit(solution)/shard_map/psum | solution.py:43
  78.8 1.2 fusion.6
  80.0 0.9 convolution_convert_fusion
  81.0 0.5 all-gather.2.cloned.1.call-update
  81.5 35.1 %all-reduce.5.cloned.1.call-done = bf16[256,512]{1,0:T(8,128)(2,1)} async-done(((bf16[256,512]{1,0:T(8,128)(2,1)}), bf16[256,512]{1,0:T(8,128)(2,1)}) %all-reduce.5.cloned.1.call-update) | async-done | bytes 262160 | tf_op jit(solution)/shard_map/psum | solution.py:43
  116.6 1.2 fusion.7
  117.8 16.0 %all_gather.6 = bf16[256,1024]{1,0:T(8,128)(2,1)S(1)} all-gather(bf16[256,256]{1,0:T(8,128)(2,1)S(1)} %fusion.7), channel_id=1, replica_groups=mesh['dp'=8,'mp'=4] {'mp'}, dimensions={1}, use_global_device_ids=true | all-gather | bytes 655360 | tf_op jit(solution)/shard_map/all_gather | solution.py:53
  133.8 2.4 %fusion.1 = bf16[256,512]{1,0:T(8,128)(2,1)} fusion(bf16[256,1024]{1,0:T(8,128)(2,1)S(1)} %all_gather.6, bf16[1024,512]{1,0:T(8,128)(2,1)} %all-gather.2.cloned.1.call-done, f32[512]{0:T(512)S(1)} %copy-done.4), kind=kOutput, calls=%fused_computation.11 | convolution fusion | flops 268828672 | bytes 1837056 | tf_op jit(solution)/shard_map/dot_general | solution.py:54
  (43 shorter events, 0.4 us)
Async XLA Ops:
  7.4 1.4 %copy-start = (bf16[1,4096,128]{2,1,0:T(8,128)(2,1)S(1)}, bf16[1,4096,128]{2,1,0:T(8,128)(2,1)}, u32[]{:S(2)}) copy-start(bf16[1,4096,128]{2,1,0:T(8,128)(2,1)} %param.11) | copy-start | bytes 3145732
  22.3 5.4 %copy-start.5 = (s32[8]{0:T(128)S(1)}, s32[8]{0:T(128)}, u32[]{:S(2)}) copy-start(s32[8]{0:T(128)} %param.12) | copy-start | bytes 100
  22.3 10.8 %all-to-all-start = ((bf16[8,2,4096]{2,1,0:T(2,128)(2,1)}), bf16[8,2,4096]{2,1,0:T(2,128)(2,1)S(1)}, u32[]{:S(2)}, u32[]{:S(2)}) async-start(bf16[8,2,4096]{2,1,0:T(2,128)(2,1)} %reshape.125), calls=%async_computation | async-start | bytes 262144 | tf_op jit(solution)/shard_map/all_to_all | solution.py:31
  27.7 51.1 %all-reduce.3.cloned.1.call-start = ((), (), s32[]{:S(2)}) async-start(), calls=%async_computation.2 | async-start | bytes 524288 | tf_op jit(solution)/shard_map/psum | solution.py:43
  33.3 11.5 %copy-start.1 = (bf16[2,256,512]{2,1,0:T(8,128)(2,1)S(1)}, bf16[2,256,512]{2,1,0:T(8,128)(2,1)}, u32[]{:S(2)}) copy-start(bf16[2,256,512]{2,1,0:T(8,128)(2,1)} %param.13) | copy-start | bytes 1572868
  44.8 34.0 %copy-start.3 = (bf16[2,256,512]{2,1,0:T(8,128)(2,1)S(1)}, bf16[2,256,512]{2,1,0:T(8,128)(2,1)}, u32[]{:S(2)}) copy-start(bf16[2,256,512]{2,1,0:T(8,128)(2,1)} %param.14) | copy-start | bytes 1572868
  45.7 0.7 copy-start.2
  45.8 70.8 %all-reduce.5.cloned.1.call-start = ((), (), s32[]{:S(2)}) async-start(), calls=%async_computation.3 | async-start | bytes 524288 | tf_op jit(solution)/shard_map/psum | solution.py:43
  81.0 52.8 %all-gather.2.cloned.1.call-start = ((), (), s32[]{:S(2)}) async-start(), calls=%async_computation.4 | async-start | bytes 1179648 | tf_op jit(solution)/shard_map/all_gather | solution.py:56
  117.8 16.0 %copy-start.4 = (f32[512]{0:T(512)S(1)}, f32[512]{0:T(512)}, u32[]{:S(2)}) copy-start(f32[512]{0:T(512)} %param.17) | copy-start | bytes 6148
Sparse Core Ops, SparseCore 0:
  45.9 32.8 all-reduce.2
  81.1 35.4 all-reduce.4
Sparse Core Ops, SparseCore 1:
  83.3 23.1 all-gather.1
where the time goes:
time: 144 us
  waiting for transfers between devices  73.4 us (51%)
  blocking collectives  26.6 us (18%)
  between operations  15.2 us (11%)
  local copies, waits for them, and re-layouts  14.7 us (10%)
  matrix products  6.65 us (5%)
  starting transfers between devices  5.45 us (4%)
  other arithmetic  1.66 us (1%)
    psum x2, waiting for transfers between devices, body(): projected = lax.psum(partial_value.astype(jnp.bfloat16), 'mp')  67.4 us
    all_gather x1, blocking collectives, body(): full_rows = lax.all_gather(crossed, 'mp', axis=1, tiled=True)  16 us
    gather x8, local copies, waits for them, and re-layouts, body(): jnp.take(tables[0], own_ids[:, hot_index], axis=0).astype(jnp.float32)  10.7 us
    all_to_all x1, blocking collectives, body(): lax.all_to_all(ordered, 'mp', split_axis=1, concat_axis=0, tiled=True)  10.6 us
    all_to_all x1, waiting for transfers between devices, body(): lax.all_to_all(pooled, 'dp', split_axis=0, concat_axis=1, tiled=True)  5.4 us
    all_to_all x1, starting transfers between devices, body(): lax.all_to_all(pooled, 'dp', split_axis=0, concat_axis=1, tiled=True)  5.33 us
  transfers between devices with their start and end apart: 4, of which 3 were waited for; matrix products, arithmetic and copies ran while one was open for 1% of the time, Pallas kernels for 0%

commit v1 on v0

--- a/solution.py
+++ b/solution.py
@@ -28,7 +28,10 @@
         summed = summed + jnp.take(tables[0], own_ids[:, hot_index], axis=0).astype(jnp.float32)
     columns = [summed.astype(jnp.bfloat16)]
     pooled = jnp.stack(columns, axis=1)
-    regrouped = lax.all_to_all(pooled, "dp", split_axis=0, concat_axis=1, tiled=True)
+    regrouped = jnp.concatenate(
+        lax.all_to_all(jnp.stack(jnp.split(pooled, lax.axis_size("dp"), axis=0)), "dp", 0, 0),
+        axis=1,
+    )
     ordered = jnp.take(regrouped, table_of_feature, axis=1)
     by_width = lax.all_to_all(ordered, "mp", split_axis=1, concat_axis=0, tiled=True)
     group_rows = by_width.shape[0]

time: 144 us -> 147 us (1.021)
  local copies, waits for them, and re-layouts: 14.7 us -> 18.2 us
    unnamed x15 -> x19, local copies, waits for them, and re-layouts: 1.47 us -> 4.88 us
where the time goes in v1:
time: 147 us; the launch traced here: 146 us
  waiting for transfers between devices  73.3 us (50%)
  blocking collectives  26.6 us (18%)
  local copies, waits for them, and re-layouts  18.2 us (12%)
  between operations  15.2 us (10%)
  matrix products  6.67 us (5%)
  starting transfers between devices  5.45 us (4%)
    psum x2, waiting for transfers between devices, body(): projected = lax.psum(partial_value.astype(jnp.bfloat16), 'mp')  67.4 us
    all_gather x1, blocking collectives, body(): full_rows = lax.all_gather(crossed, 'mp', axis=1, tiled=True)  16 us
    gather x8, local copies, waits for them, and re-layouts, body(): jnp.take(tables[0], own_ids[:, hot_index], axis=0).astype(jnp.float32)  10.7 us
    all_to_all x1, blocking collectives, body(): lax.all_to_all(ordered, 'mp', split_axis=1, concat_axis=0, tiled=True)  10.6 us
    all_to_all x1, waiting for transfers between devices, body(): lax.all_to_all(jnp.stack(jnp.split(pooled, lax.axis_size('dp'), axis=0)),...  5.4 us
    all_to_all x1, starting transfers between devices, body(): lax.all_to_all(jnp.stack(jnp.split(pooled, lax.axis_size('dp'), axis=0)),...  5.33 us
    unnamed x19, local copies, waits for them, and re-layouts  4.88 us
  transfers between devices with their start and end apart: 4, of which 3 were waited for; matrix products, arithmetic and copies ran while one was open for 1% of the time, Pallas kernels for 0%

profile of v1, /device:TPU:0, one launch (start us, length us, event | category | flops | bytes accessed | tf_op | source)
XLA Modules:
  0.0 146.3 jit_solution(5905630463273590076)
XLA Ops:
  7.4 1.0 reshape_squeeze.3
  8.8 1.3 gather_fusion.2
  10.2 1.3 gather_fusion.3
  11.5 1.3 gather_fusion.4
  12.9 1.3 gather_fusion.5
  14.2 1.3 gather_fusion.6
  15.6 1.3 gather_fusion.1
  16.9 1.3 gather_fusion.7
  18.3 1.3 gather_fusion.8
  19.6 0.8 add_convert_fusion
  20.4 0.6 fusion.25
  21.0 0.6 fusion.24
  21.6 0.6 fusion.23
  22.2 0.6 fusion.22
  22.8 0.6 fusion.21
  23.4 0.6 fusion.20
  24.1 0.6 fusion.19
  24.7 0.6 fusion.18
  25.3 5.3 %all-to-all-start = ((bf16[8,64,1,128]{3,1,2,0:T(8,128)(2,1)}), bf16[8,64,1,128]{3,1,2,0:T(8,128)(2,1)S(1)}, u32[]{:S(2)}, u32[]{:S(2)}) async-start(bf16[8,64,1,128]{3,1,2,0:T(8,128)(2,1)} %fusion.18), calls=%async_computation | async-start | bytes 262144 | tf_op jit(solution)/shard_map/all_to_all | solution.py:32
  30.7 5.4 %all-to-all-done = bf16[8,64,1,128]{3,1,2,0:T(8,128)(2,1)S(1)} async-done(((bf16[8,64,1,128]{3,1,2,0:T(8,128)(2,1)}), bf16[8,64,1,128]{3,1,2,0:T(8,128)(2,1)S(1)}, u32[]{:S(2)}, u32[]{:S(2)}) %all-to-all-start) | async-done | bytes 131104 | tf_op jit(solution)/shard_map/all_to_all | solution.py:32
  36.1 0.6 gather_fusion
  36.8 10.6 %all_to_all.20 = bf16[64,8,128]{2,0,1:T(8,128)(2,1)S(1)} all-to-all(bf16[64,8,128]{2,0,1:T(8,128)(2,1)S(1)} %select_bitcast_fusion), channel_id=1, replica_groups=mesh['dp'=8,'mp'=4] {'mp'}, dimensions={1} | all-to-all | bytes 262144 | tf_op jit(solution)/shard_map/all_to_all | solution.py:36
  47.6 0.9 convolution_convert_fusion.1
  48.6 0.6 copy-done.2
  49.2 32.3 %all-reduce.3.cloned.1.call-done = bf16[256,512]{1,0:T(8,128)(2,1)} async-done(((bf16[256,512]{1,0:T(8,128)(2,1)}), bf16[256,512]{1,0:T(8,128)(2,1)}) %all-reduce.3.cloned.1.call-update) | async-done | bytes 262160 | tf_op jit(solution)/shard_map/psum | solution.py:46
  81.5 1.2 fusion.6
  82.8 0.9 convolution_convert_fusion
  83.8 0.5 all-gather.2.cloned.1.call-update
  84.3 35.0 %all-reduce.5.cloned.1.call-done = bf16[256,512]{1,0:T(8,128)(2,1)} async-done(((bf16[256,512]{1,0:T(8,128)(2,1)}), bf16[256,512]{1,0:T(8,128)(2,1)}) %all-reduce.5.cloned.1.call-update) | async-done | bytes 262160 | tf_op jit(solution)/shard_map/psum | solution.py:46
  119.3 1.2 fusion.7
  120.6 16.0 %all_gather.6 = bf16[256,1024]{1,0:T(8,128)(2,1)S(1)} all-gather(bf16[256,256]{1,0:T(8,128)(2,1)S(1)} %fusion.7), channel_id=1, replica_groups=mesh['dp'=8,'mp'=4] {'mp'}, dimensions={1}, use_global_device_ids=true | all-gather | bytes 655360 | tf_op jit(solution)/shard_map/all_gather | solution.py:56
  136.5 2.4 %fusion.1 = bf16[256,512]{1,0:T(8,128)(2,1)} fusion(bf16[256,1024]{1,0:T(8,128)(2,1)S(1)} %all_gather.6, bf16[1024,512]{1,0:T(8,128)(2,1)} %all-gather.2.cloned.1.call-done, f32[512]{0:T(512)S(1)} %copy-done.4), kind=kOutput, calls=%fused_computation.11 | convolution fusion | flops 268828672 | bytes 1837056 | tf_op jit(solution)/shard_map/dot_general | solution.py:57
  (42 shorter events, 0.7 us)
Async XLA Ops:
  7.4 1.4 copy-start
  25.3 5.4 %copy-start.5 = (s32[8]{0:T(128)S(1)}, s32[8]{0:T(128)}, u32[]{:S(2)}) copy-start(s32[8]{0:T(128)} %param.12) | copy-start | bytes 100
  25.3 10.8 %all-to-all-start = ((bf16[8,64,1,128]{3,1,2,0:T(8,128)(2,1)}), bf16[8,64,1,128]{3,1,2,0:T(8,128)(2,1)S(1)}, u32[]{:S(2)}, u32[]{:S(2)}) async-start(bf16[8,64,1,128]{3,1,2,0:T(8,128)(2,1)} %fusion.18), calls=%async_computation | async-start | bytes 262144 | tf_op jit(solution)/shard_map/all_to_all | solution.py:32
  30.6 50.9 %all-reduce.3.cloned.1.call-start = ((), (), s32[]{:S(2)}) async-start(), calls=%async_computation.2 | async-start | bytes 524288 | tf_op jit(solution)/shard_map/psum | solution.py:46
  36.1 11.5 %copy-start.1 = (bf16[2,256,512]{2,1,0:T(8,128)(2,1)S(1)}, bf16[2,256,512]{2,1,0:T(8,128)(2,1)}, u32[]{:S(2)}) copy-start(bf16[2,256,512]{2,1,0:T(8,128)(2,1)} %param.13) | copy-start | bytes 1572868
  47.5 34.0 %copy-start.3 = (bf16[2,256,512]{2,1,0:T(8,128)(2,1)S(1)}, bf16[2,256,512]{2,1,0:T(8,128)(2,1)}, u32[]{:S(2)}) copy-start(bf16[2,256,512]{2,1,0:T(8,128)(2,1)} %param.14) | copy-start | bytes 1572868
  48.5 0.7 copy-start.2
  48.5 70.8 %all-reduce.5.cloned.1.call-start = ((), (), s32[]{:S(2)}) async-start(), calls=%async_computation.3 | async-start | bytes 524288 | tf_op jit(solution)/shard_map/psum | solution.py:46
  83.7 52.8 %all-gather.2.cloned.1.call-start = ((), (), s32[]{:S(2)}) async-start(), calls=%async_computation.4 | async-start | bytes 1179648 | tf_op jit(solution)/shard_map/all_gather | solution.py:59
  120.6 16.0 %copy-start.4 = (f32[512]{0:T(512)S(1)}, f32[512]{0:T(512)}, u32[]{:S(2)}) copy-start(f32[512]{0:T(512)} %param.17) | copy-start | bytes 6148
Sparse Core Ops, SparseCore 0:
  48.7 32.8 all-reduce.2
  83.9 35.4 all-reduce.4
Sparse Core Ops, SparseCore 1:
  86.1 23.1 all-gather.1
